TPU v7x, 128 devices: a whole 4x4x4 slice. The times are simulated.
128 devices in a mesh: seq: 4 (over z_lo, core), mp: 32 (over z_hi, y, x).
Axes of the slice: x: 4, y: 4, z: 4 (z_hi: 2, z_lo: 2; z = z_hi * 2 + z_lo), core: 2. Of those that a mesh axis runs over, the one named last changes fastest.
Arguments:
- byte_states: bfloat16 [4, 16384, 1024], P('seq', 'mp'), may hold values from -312 to 312
- patch_latents: bfloat16 [4, 4096, 4096], P(None, 'seq', 'mp'), may hold values from -6 to 6
- patch_lengths: int32 [4, 4096], P('seq'), may hold values from 1 to 12, 16384 in all within a row
- w_down: bfloat16 [4096, 1024], replicated, may hold values from -0.09375 to 0.09375
- kv_gain: bfloat16 [1024], replicated, may hold values from 0.25 to 1.75
- w_query: bfloat16 [1024, 1024], replicated, may hold values from -0.375 to 0.375
- w_key: bfloat16 [1024, 1024], replicated, may hold values from -0.1875 to 0.1875
- w_value: bfloat16 [1024, 1024], replicated, may hold values from -0.1875 to 0.1875
- w_out: bfloat16 [1024, 1024], replicated, may hold values from -0.375 to 0.375
- out_gain: bfloat16 [1024], replicated, may hold values from 0.25 to 1.75
Outputs:
- decoded: bfloat16 [4, 16384, 1024], P('seq', 'mp')
Inputs may be any that keep to these rules, and one draw needn't show every extreme that they name: patch_lengths[s] lists the lengths of the 4096 patches of sequence s in order; they sum to 16384 and the longest is exactly 12.
All inputs are finite; a program needn't handle non-finite values.
Results may differ from a plain program's by a relative error of at most 0.0076.
Values may be sent and summed in bfloat16 or wider, within the bound.
No kernel may reach another device: no remote copies, remote signals or barrier semaphores. Data moves between devices by JAX's collectives and lax.ppermute only.
A program may use at most 128 MiB of HBM per device.

v0:
```python
import math
import jax
import jax.numpy as jnp
from jax import lax
from jax.sharding import PartitionSpec as P

HEADS = 16
HEAD_DIM = 64
NEG_FLOOR = -1e30


def from_partner(value, axis, apart):
    mask = 2**apart
    pairs = [(source, source ^ mask) for source in range(lax.axis_size(axis))]
    return lax.ppermute(value, axis, pairs)


def in_one_piece(arrays, axis, dim, along):
    both = jnp.concatenate(arrays, axis=along)
    filled, at, finished = (lax.all_gather(both, axis, axis=dim, tiled=True), 0, [])
    for a in arrays:
        finished.append(lax.slice_in_dim(filled, at, at + a.shape[along], axis=along))
        at += a.shape[along]
    return tuple(finished)


def rms_norm(values, gain_row):
    mean_square = jnp.mean(values * values, axis=-1, keepdims=True)
    return values * lax.rsqrt(mean_square + 1e-05) * gain_row.astype(jnp.float32)


def fold_block(fold_state, query_part, position_part, key_block, value_block, start_block):
    row_max, denominator, accumulated = fold_state
    scale_factor = 1.0 / math.sqrt(HEAD_DIM)
    scores = (
        jnp.einsum("rhd,khd->hrk", query_part, key_block, preferred_element_type=jnp.float32)
        * scale_factor
    )
    allowed = start_block[None, None, :] <= position_part[None, :, None]
    masked = jnp.where(allowed, scores, NEG_FLOOR)
    new_max = jnp.maximum(row_max, jnp.max(masked, axis=-1))
    raised = jnp.where(allowed, jnp.exp(masked - new_max[..., None]), 0.0)
    correction = jnp.exp(row_max - new_max)
    denominator = denominator * correction + jnp.sum(raised, axis=-1)
    accumulated = accumulated * correction[..., None] + jnp.einsum(
        "hrk,khd->hrd", raised.astype(jnp.bfloat16), value_block, preferred_element_type=jnp.float32
    )
    return (new_max, denominator, accumulated)


def make_folder(query_halves, position_halves, starts):

    def folder(running, arrived_piece, piece_start):
        key_piece, value_piece = arrived_piece
        piece_rows = key_piece.shape[0]
        step_rows = math.gcd(piece_rows, 512)

        def one_block(block_index, fold_state):
            offset = block_index * step_rows
            key_block = lax.dynamic_slice_in_dim(key_piece, offset, step_rows, 0).reshape(
                step_rows, HEADS, HEAD_DIM
            )
            value_block = lax.dynamic_slice_in_dim(value_piece, offset, step_rows, 0).reshape(
                step_rows, HEADS, HEAD_DIM
            )
            start_block = lax.dynamic_slice_in_dim(starts, offset, step_rows, 0)
            updated = []
            for part_index in range(2):
                part_state = tuple((member[part_index] for member in fold_state))

                def advance(inner_state, part_index=part_index):
                    return fold_block(
                        inner_state,
                        query_halves[part_index],
                        position_halves[part_index],
                        key_block,
                        value_block,
                        start_block,
                    )

                def remain(inner_state):
                    return inner_state

                needed = start_block[0] <= position_halves[part_index][-1]
                updated.append(lax.cond(needed, advance, remain, part_state))
            return tuple((jnp.stack([updated[0][slot], updated[1][slot]]) for slot in range(3)))

        return lax.fori_loop(0, piece_rows // step_rows, one_block, running)

    return folder


def per_device(
    byte_states,
    patch_latents,
    patch_lengths,
    w_down,
    kv_gain,
    w_query,
    w_key,
    w_value,
    w_out,
    out_gain,
):
    mp_count = lax.axis_size("mp")
    my_rank = lax.axis_index("mp")
    tokens_here = byte_states.shape[1]
    half_rows = tokens_here // 2
    regrouped = lax.all_to_all(
        lax.all_to_all(patch_latents, "seq", split_axis=0, concat_axis=1, tiled=True),
        "mp",
        split_axis=1,
        concat_axis=2,
        tiled=True,
    )
    projected = jnp.dot(regrouped[0], w_down, preferred_element_type=jnp.float32)
    patch_normed = rms_norm(projected, kv_gain).astype(jnp.bfloat16)
    lengths = patch_lengths[0]
    starts = jnp.cumsum(lengths) - lengths
    own_rows = byte_states[0]
    local_offsets = jnp.arange(half_rows, dtype=jnp.int32)
    first_position = my_rank * tokens_here
    top_bit = mp_count.bit_length() - 2
    partner = jnp.bitwise_xor(my_rank, mp_count // 2)
    arrived_rows = from_partner(own_rows[half_rows:], "mp", top_bit)
    work_rows = jnp.concatenate([own_rows[:half_rows], arrived_rows], axis=0)
    position_halves = jnp.stack(
        [first_position + local_offsets, partner * tokens_here + half_rows + local_offsets]
    )
    queries = jnp.dot(work_rows, w_query, preferred_element_type=jnp.float32).astype(jnp.bfloat16)
    query_halves = queries.reshape(2, half_rows, HEADS, HEAD_DIM)
    initial = (
        jnp.full((2, HEADS, half_rows), NEG_FLOOR, jnp.float32),
        jnp.zeros((2, HEADS, half_rows), jnp.float32),
        jnp.zeros((2, HEADS, half_rows, HEAD_DIM), jnp.float32),
    )
    key_rows = jnp.dot(patch_normed, w_key, preferred_element_type=jnp.float32).astype(jnp.bfloat16)
    value_rows = jnp.dot(patch_normed, w_value, preferred_element_type=jnp.float32).astype(
        jnp.bfloat16
    )
    folder = make_folder(query_halves, position_halves, starts)
    row_max, denominator, accumulated = folder(
        initial, in_one_piece((key_rows, value_rows), "mp", 0, 1), jnp.int32(0)
    )
    summed = accumulated / denominator[..., None]
    head_out = (
        jnp.transpose(summed, (0, 2, 1, 3))
        .reshape(tokens_here, HEADS * HEAD_DIM)
        .astype(jnp.bfloat16)
    )
    residual = work_rows.astype(jnp.float32) + jnp.dot(
        head_out, w_out, preferred_element_type=jnp.float32
    )
    decoded = rms_norm(residual, out_gain).astype(jnp.bfloat16)
    returned = from_partner(decoded[half_rows:], "mp", top_bit)
    decoded = jnp.concatenate([decoded[:half_rows], returned], axis=0)
    return decoded[None]


def solution(mesh):
    return jax.shard_map(
        per_device,
        mesh=mesh,
        in_specs=(
            P("seq", "mp", None),
            P(None, "seq", "mp"),
            P("seq", None),
            P(),
            P(),
            P(),
            P(),
            P(),
            P(),
            P(),
        ),
        out_specs=P("seq", "mp", None),
        check_vma=False,
    )
```

profile of v0, /device:TPU:24, one launch (start us, length us, event | category | flops | bytes accessed | tf_op | source)
XLA Modules:
  0.0 601.6 jit_solution(1319241090054931026)
XLA Ops:
  6.5 18.0 %all_to_all.27 = bf16[4,1024,128]{2,1,0:T(8,128)(2,1)S(1)} all-to-all(bf16[4,1024,128]{2,1,0:T(8,128)(2,1)} %param.17), channel_id=1, replica_groups=mesh['seq'=4,'mp'=32] {'seq'}, dimensions={0} | all-to-all | bytes 2097152 | tf_op jit(solution)/shard_map/all_to_all | solution.py:110
  24.6 17.0 %copy.45 = bf16[1,4096,128]{2,0,1:T(2,128)(2,1)} copy(bf16[1,4096,128]{2,1,0:T(8,128)(2,1)S(1)} %bitcast.101) | data formatting | bytes 2097152 | tf_op jit(solution)/shard_map/all_to_all | solution.py:110
  42.1 23.4 %reduce.2 = bf16[4096,128]{1,0:T(8,128)(2,1)S(1)} reduce(bf16[4096,1,128]{2,1,0:T(2,128)(2,1)} %bitcast.98, bf16[]{:T(256)} %broadcast.104), dimensions={1}, to_apply=%bitcast.78.reduce_sub_computation | reduce | bytes 2097154
  66.7 10.6 %all-to-all-start.1 = ((bf16[32,2,8192]{2,1,0:T(2,128)(2,1)}), bf16[32,2,8192]{2,1,0:T(2,128)(2,1)S(1)}, u32[]{:S(2)}, u32[]{:S(2)}) async-start(bf16[32,2,8192]{2,1,0:T(2,128)(2,1)} %reshape.140), calls=%async_computation.1 | async-start | bytes 2097152 | tf_op jit(solution)/shard_map/all_to_all | solution.py:109
  77.5 16.8 %all-to-all-done.1 = bf16[32,2,8192]{2,1,0:T(2,128)(2,1)S(1)} async-done(((bf16[32,2,8192]{2,1,0:T(2,128)(2,1)}), bf16[32,2,8192]{2,1,0:T(2,128)(2,1)S(1)}, u32[]{:S(2)}, u32[]{:S(2)}) %all-to-all-start.1) | async-done | bytes 1048608 | tf_op jit(solution)/shard_map/all_to_all | solution.py:109
  94.4 3.5 reshape.141
  102.2 4.9 multiply_reduce_fusion.1
  112.3 15.8 %collective-permute-done = bf16[256,1024]{1,0:T(8,128)(2,1)S(1)} collective-permute-done((bf16[256,1024]{1,0:T(8,128)(2,1)}, bf16[256,1024]{1,0:T(8,128)(2,1)S(1)}, u32[]{:S(2)}, u32[]{:S(2)}) %collective-permute-start) | collective-permute-done | bytes 524320 | tf_op jit(solution)/shard_map/ppermute | solution.py:15
  128.1 4.0 convolution_convert_fusion
  132.1 4.0 reshape.138
  136.1 3.5 copy.36
  139.6 123.1 %all-gather.2.cloned.1.call-done = bf16[4096,2048]{1,0:T(8,128)(2,1)} async-done(((bf16[128,2048]{1,0:T(8,128)(2,1)}), bf16[4096,2048]{1,0:T(8,128)(2,1)}) %all-gather.2.cloned.1.call-update) | async-done | bytes 16777232 | tf_op jit(solution)/shard_map/all_gather | solution.py:20
  262.7 11.6 %fusion.38 = (bf16[4096,1024]{1,0:T(8,128)(2,1)}, bf16[4096,1024]{1,0:T(8,128)(2,1)}) fusion(bf16[4096,2048]{1,0:T(8,128)(2,1)} %all-gather.2.cloned.1.call-done), kind=kLoop, calls=%fused_computation.69 | loop fusion | bytes 33554432 | tf_op jit(solution)/shard_map/slice | solution.py:22
  275.9 297.0 %while.17 = (s32[]{:T(128)}, f32[2,16,256]{2,1,0:T(8,128)S(1)}, f32[2,16,256]{2,1,0:T(8,128)S(1)}, f32[2,16,256,64]{2,3,1,0:T(8,128)}, s32[4096]{0:T(1024)S(1)},...) while((s32[]{:T(128)}, f32[2,16,256]{2,1,0:T(8,128)S(1)}, ...), condition=%wide.region_12.13_spmd, body=%wide.region_3.12_spmd.sunk | while | flops 1130135552 | bytes 99363408 | solution.py:88
  289.4 10.8 %conditional.5 = (f32[1,16,256]{2,1,0:T(8,128)}, f32[1,16,256]{2,1,0:T(8,128)S(1)}, f32[1,16,256,64]{2,3,1,0:T(8,128)S(1)}) conditional(s32[]{:T(128)} %bitcast.90, (f32[16,256]{1,0:T(8,128)}, f32[16,256]{1,0:T(8,128)S(1)}, f32[16,256,64]{1,2,0:T(8,128)S(1)}) %tuple.134, (s32[512]{0:T(512)S(1)}, s32[256]{0:T(256)S(1)}, ...), branch_computations={%region_4.4_spmd, %region_5.0_spmd} | conditional | flops 564797440 | bytes 34835508 | solution.py:85
  302.8 11.9 %conditional.4 = (f32[1,16,256]{2,1,0:T(8,128)}, f32[1,16,256]{2,1,0:T(8,128)S(1)}, f32[1,16,256,64]{2,3,1,0:T(8,128)}) conditional(s32[]{:T(128)} %bitcast.87, (f32[16,256]{1,0:T(8,128)}, f32[16,256]{1,0:T(8,128)S(1)}, f32[16,256,64]{1,2,0:T(8,128)}) %tuple.132, (s32[512]{0:T(512)S(1)}, s32[256]{0:T(256)S(1)}, bf16[2,256,16,64]{1,3,2,0:T(8,128)(2,1)}, ...), branch_computations={%region_8.8_spmd, %region_9.0_spmd} | conditional | flops 564797440 | bytes 43224172 | solution.py:85
  306.5 3.2 fusion.20
  331.9 10.8 %conditional.5 = (f32[1,16,256]{2,1,0:T(8,128)}, f32[1,16,256]{2,1,0:T(8,128)S(1)}, f32[1,16,256,64]{2,3,1,0:T(8,128)S(1)}) conditional(s32[]{:T(128)} %bitcast.90, (f32[16,256]{1,0:T(8,128)}, f32[16,256]{1,0:T(8,128)S(1)}, f32[16,256,64]{1,2,0:T(8,128)S(1)}) %tuple.134, (s32[512]{0:T(512)S(1)}, s32[256]{0:T(256)S(1)}, ...), branch_computations={%region_4.4_spmd, %region_5.0_spmd} | conditional | flops 564797440 | bytes 34835508 | solution.py:85
  335.6 3.2 fusion.2
  345.3 11.9 %conditional.4 = (f32[1,16,256]{2,1,0:T(8,128)}, f32[1,16,256]{2,1,0:T(8,128)S(1)}, f32[1,16,256,64]{2,3,1,0:T(8,128)}) conditional(s32[]{:T(128)} %bitcast.87, (f32[16,256]{1,0:T(8,128)}, f32[16,256]{1,0:T(8,128)S(1)}, f32[16,256,64]{1,2,0:T(8,128)}) %tuple.132, (s32[512]{0:T(512)S(1)}, s32[256]{0:T(256)S(1)}, bf16[2,256,16,64]{1,3,2,0:T(8,128)(2,1)}, ...), branch_computations={%region_8.8_spmd, %region_9.0_spmd} | conditional | flops 564797440 | bytes 43224172 | solution.py:85
  349.0 3.2 fusion.20
  374.4 10.8 %conditional.5 = (f32[1,16,256]{2,1,0:T(8,128)}, f32[1,16,256]{2,1,0:T(8,128)S(1)}, f32[1,16,256,64]{2,3,1,0:T(8,128)S(1)}) conditional(s32[]{:T(128)} %bitcast.90, (f32[16,256]{1,0:T(8,128)}, f32[16,256]{1,0:T(8,128)S(1)}, f32[16,256,64]{1,2,0:T(8,128)S(1)}) %tuple.134, (s32[512]{0:T(512)S(1)}, s32[256]{0:T(256)S(1)}, ...), branch_computations={%region_4.4_spmd, %region_5.0_spmd} | conditional | flops 564797440 | bytes 34835508 | solution.py:85
  387.8 11.9 %conditional.4 = (f32[1,16,256]{2,1,0:T(8,128)}, f32[1,16,256]{2,1,0:T(8,128)S(1)}, f32[1,16,256,64]{2,3,1,0:T(8,128)}) conditional(s32[]{:T(128)} %bitcast.87, (f32[16,256]{1,0:T(8,128)}, f32[16,256]{1,0:T(8,128)S(1)}, f32[16,256,64]{1,2,0:T(8,128)}) %tuple.132, (s32[512]{0:T(512)S(1)}, s32[256]{0:T(256)S(1)}, bf16[2,256,16,64]{1,3,2,0:T(8,128)(2,1)}, ...), branch_computations={%region_8.8_spmd, %region_9.0_spmd} | conditional | flops 564797440 | bytes 43224172 | solution.py:85
  416.9 10.8 %conditional.5 = (f32[1,16,256]{2,1,0:T(8,128)}, f32[1,16,256]{2,1,0:T(8,128)S(1)}, f32[1,16,256,64]{2,3,1,0:T(8,128)S(1)}) conditional(s32[]{:T(128)} %bitcast.90, (f32[16,256]{1,0:T(8,128)}, f32[16,256]{1,0:T(8,128)S(1)}, f32[16,256,64]{1,2,0:T(8,128)S(1)}) %tuple.134, (s32[512]{0:T(512)S(1)}, s32[256]{0:T(256)S(1)}, ...), branch_computations={%region_4.4_spmd, %region_5.0_spmd} | conditional | flops 564797440 | bytes 34835508 | solution.py:85
  420.6 3.2 fusion.2
  430.3 11.9 %conditional.4 = (f32[1,16,256]{2,1,0:T(8,128)}, f32[1,16,256]{2,1,0:T(8,128)S(1)}, f32[1,16,256,64]{2,3,1,0:T(8,128)}) conditional(s32[]{:T(128)} %bitcast.87, (f32[16,256]{1,0:T(8,128)}, f32[16,256]{1,0:T(8,128)S(1)}, f32[16,256,64]{1,2,0:T(8,128)}) %tuple.132, (s32[512]{0:T(512)S(1)}, s32[256]{0:T(256)S(1)}, bf16[2,256,16,64]{1,3,2,0:T(8,128)(2,1)}, ...), branch_computations={%region_8.8_spmd, %region_9.0_spmd} | conditional | flops 564797440 | bytes 43224172 | solution.py:85
  434.0 3.2 fusion.20
  462.0 11.9 %conditional.4 = (f32[1,16,256]{2,1,0:T(8,128)}, f32[1,16,256]{2,1,0:T(8,128)S(1)}, f32[1,16,256,64]{2,3,1,0:T(8,128)}) conditional(s32[]{:T(128)} %bitcast.87, (f32[16,256]{1,0:T(8,128)}, f32[16,256]{1,0:T(8,128)S(1)}, f32[16,256,64]{1,2,0:T(8,128)}) %tuple.132, (s32[512]{0:T(512)S(1)}, s32[256]{0:T(256)S(1)}, bf16[2,256,16,64]{1,3,2,0:T(8,128)(2,1)}, ...), branch_computations={%region_8.8_spmd, %region_9.0_spmd} | conditional | flops 564797440 | bytes 43224172 | solution.py:85
  493.7 11.9 %conditional.4 = (f32[1,16,256]{2,1,0:T(8,128)}, f32[1,16,256]{2,1,0:T(8,128)S(1)}, f32[1,16,256,64]{2,3,1,0:T(8,128)}) conditional(s32[]{:T(128)} %bitcast.87, (f32[16,256]{1,0:T(8,128)}, f32[16,256]{1,0:T(8,128)S(1)}, f32[16,256,64]{1,2,0:T(8,128)}) %tuple.132, (s32[512]{0:T(512)S(1)}, s32[256]{0:T(256)S(1)}, bf16[2,256,16,64]{1,3,2,0:T(8,128)(2,1)}, ...), branch_computations={%region_8.8_spmd, %region_9.0_spmd} | conditional | flops 564797440 | bytes 43224172 | solution.py:85
  525.5 11.9 %conditional.4 = (f32[1,16,256]{2,1,0:T(8,128)}, f32[1,16,256]{2,1,0:T(8,128)S(1)}, f32[1,16,256,64]{2,3,1,0:T(8,128)}) conditional(s32[]{:T(128)} %bitcast.87, (f32[16,256]{1,0:T(8,128)}, f32[16,256]{1,0:T(8,128)S(1)}, f32[16,256,64]{1,2,0:T(8,128)}) %tuple.132, (s32[512]{0:T(512)S(1)}, s32[256]{0:T(256)S(1)}, bf16[2,256,16,64]{1,3,2,0:T(8,128)(2,1)}, ...), branch_computations={%region_8.8_spmd, %region_9.0_spmd} | conditional | flops 564797440 | bytes 43224172 | solution.py:85
  557.2 11.9 %conditional.4 = (f32[1,16,256]{2,1,0:T(8,128)}, f32[1,16,256]{2,1,0:T(8,128)S(1)}, f32[1,16,256,64]{2,3,1,0:T(8,128)}) conditional(s32[]{:T(128)} %bitcast.87, (f32[16,256]{1,0:T(8,128)}, f32[16,256]{1,0:T(8,128)S(1)}, f32[16,256,64]{1,2,0:T(8,128)}) %tuple.132, (s32[512]{0:T(512)S(1)}, s32[256]{0:T(256)S(1)}, bf16[2,256,16,64]{1,3,2,0:T(8,128)(2,1)}, ...), branch_computations={%region_8.8_spmd, %region_9.0_spmd} | conditional | flops 564797440 | bytes 43224172 | solution.py:85
  579.3 14.4 %collective-permute-done.1 = bf16[256,1024]{1,0:T(8,128)(2,1)S(1)} collective-permute-done((bf16[256,1024]{1,0:T(8,128)(2,1)S(1)}, bf16[256,1024]{1,0:T(8,128)(2,1)S(1)}, u32[]{:S(2)}, u32[]{:S(2)}) %collective-permute-start.1) | collective-permute-done | bytes 524320 | tf_op jit(solution)/shard_map/ppermute | solution.py:15
  (307 shorter events, 279.6 us)
Async XLA Ops:
  6.5 569.6 %copy-start = (bf16[1024,1024]{1,0:T(8,128)(2,1)S(1)}, bf16[1024,1024]{1,0:T(8,128)(2,1)}, u32[]{:S(2)}) copy-start(bf16[1024,1024]{1,0:T(8,128)(2,1)} %param.24) | copy-start | bytes 6291460
  6.5 71.0 %copy-start.13 = (bf16[1024]{0:T(1024)(128)(2,1)S(1)}, bf16[1024]{0:T(1024)(128)(2,1)}, u32[]{:S(2)}) copy-start(bf16[1024]{0:T(1024)(128)(2,1)} %param.20) | copy-start | bytes 6148
  66.7 27.7 %all-to-all-start.1 = ((bf16[32,2,8192]{2,1,0:T(2,128)(2,1)}), bf16[32,2,8192]{2,1,0:T(2,128)(2,1)S(1)}, u32[]{:S(2)}, u32[]{:S(2)}) async-start(bf16[32,2,8192]{2,1,0:T(2,128)(2,1)} %reshape.140), calls=%async_computation.1 | async-start | bytes 2097152 | tf_op jit(solution)/shard_map/all_to_all | solution.py:109
  77.3 185.4 %all-gather.2.cloned.1.call-start = ((), (), s32[]{:S(2)}) async-start(), calls=%async_computation.2 | async-start | bytes 17301504 | tf_op jit(solution)/shard_map/all_gather | solution.py:20
  102.2 5.0 copy-start.10
  102.2 5.5 copy-start.11
  111.1 28.5 %copy-start.6 = (bf16[256,1024]{1,0:T(8,128)(2,1)}, bf16[256,1024]{1,0:T(8,128)(2,1)S(1)}, u32[]{:S(2)}) copy-start(bf16[256,1024]{1,0:T(8,128)(2,1)S(1)} %get-tuple-element.383) | copy-start | bytes 1572868
  111.1 17.0 %collective-permute-start = (bf16[256,1024]{1,0:T(8,128)(2,1)}, bf16[256,1024]{1,0:T(8,128)(2,1)S(1)}, u32[]{:S(2)}, u32[]{:S(2)}) collective-permute-start(bf16[256,1024]{1,0:T(8,128)(2,1)} %get-tuple-element.384), channel_id=1, source_target_pairs={{0,16},{1,17},{2,18},{3,19},{4,20},{5,21},{6,22},{7,23},{8,24},{9,... | collective-permute-start | bytes 1572872 | tf_op jit(solution)/shard_map/ppermute | solution.py:15
  128.1 146.3 %copy-start.8 = (bf16[256,1024]{1,0:T(8,128)(2,1)}, bf16[256,1024]{1,0:T(8,128)(2,1)S(1)}, u32[]{:S(2)}) copy-start(bf16[256,1024]{1,0:T(8,128)(2,1)S(1)} %collective-permute-done) | copy-start | bytes 1572868
  289.6 7.5 %copy-start.4 = (bf16[512,16,64]{0,2,1:T(8,128)(2,1)S(1)}, bf16[512,16,64]{0,2,1:T(8,128)(2,1)}, u32[]{:S(2)}) copy-start(bf16[512,16,64]{0,2,1:T(8,128)(2,1)} %get-tuple-element.249) | copy-start | bytes 3145732 | tf_op jit(solution)/shard_map/while/body/eval_jaxpr/cond
  302.9 7.5 %copy-start.1 = (f32[16,256,64]{1,2,0:T(8,128)S(1)}, f32[16,256,64]{1,2,0:T(8,128)}, u32[]{:S(2)}) copy-start(f32[16,256,64]{1,2,0:T(8,128)} %get-tuple-element.256) | copy-start | bytes 3145732 | tf_op jit(solution)/shard_map/while/body/eval_jaxpr/cond
  302.9 7.5 %copy-start.5 = (bf16[512,16,64]{0,2,1:T(8,128)(2,1)S(1)}, bf16[512,16,64]{0,2,1:T(8,128)(2,1)}, u32[]{:S(2)}) copy-start(bf16[512,16,64]{0,2,1:T(8,128)(2,1)} %get-tuple-element.257) | copy-start | bytes 3145732 | tf_op jit(solution)/shard_map/while/body/eval_jaxpr/cond
  332.1 7.5 %copy-start.4 = (bf16[512,16,64]{0,2,1:T(8,128)(2,1)S(1)}, bf16[512,16,64]{0,2,1:T(8,128)(2,1)}, u32[]{:S(2)}) copy-start(bf16[512,16,64]{0,2,1:T(8,128)(2,1)} %get-tuple-element.249) | copy-start | bytes 3145732 | tf_op jit(solution)/shard_map/while/body/eval_jaxpr/cond
  345.4 7.5 %copy-start.1 = (f32[16,256,64]{1,2,0:T(8,128)S(1)}, f32[16,256,64]{1,2,0:T(8,128)}, u32[]{:S(2)}) copy-start(f32[16,256,64]{1,2,0:T(8,128)} %get-tuple-element.256) | copy-start | bytes 3145732 | tf_op jit(solution)/shard_map/while/body/eval_jaxpr/cond
  345.4 7.5 %copy-start.5 = (bf16[512,16,64]{0,2,1:T(8,128)(2,1)S(1)}, bf16[512,16,64]{0,2,1:T(8,128)(2,1)}, u32[]{:S(2)}) copy-start(bf16[512,16,64]{0,2,1:T(8,128)(2,1)} %get-tuple-element.257) | copy-start | bytes 3145732 | tf_op jit(solution)/shard_map/while/body/eval_jaxpr/cond
  374.6 7.5 %copy-start.4 = (bf16[512,16,64]{0,2,1:T(8,128)(2,1)S(1)}, bf16[512,16,64]{0,2,1:T(8,128)(2,1)}, u32[]{:S(2)}) copy-start(bf16[512,16,64]{0,2,1:T(8,128)(2,1)} %get-tuple-element.249) | copy-start | bytes 3145732 | tf_op jit(solution)/shard_map/while/body/eval_jaxpr/cond
  387.9 7.5 %copy-start.1 = (f32[16,256,64]{1,2,0:T(8,128)S(1)}, f32[16,256,64]{1,2,0:T(8,128)}, u32[]{:S(2)}) copy-start(f32[16,256,64]{1,2,0:T(8,128)} %get-tuple-element.256) | copy-start | bytes 3145732 | tf_op jit(solution)/shard_map/while/body/eval_jaxpr/cond
  387.9 7.5 %copy-start.5 = (bf16[512,16,64]{0,2,1:T(8,128)(2,1)S(1)}, bf16[512,16,64]{0,2,1:T(8,128)(2,1)}, u32[]{:S(2)}) copy-start(bf16[512,16,64]{0,2,1:T(8,128)(2,1)} %get-tuple-element.257) | copy-start | bytes 3145732 | tf_op jit(solution)/shard_map/while/body/eval_jaxpr/cond
  417.1 7.5 %copy-start.4 = (bf16[512,16,64]{0,2,1:T(8,128)(2,1)S(1)}, bf16[512,16,64]{0,2,1:T(8,128)(2,1)}, u32[]{:S(2)}) copy-start(bf16[512,16,64]{0,2,1:T(8,128)(2,1)} %get-tuple-element.249) | copy-start | bytes 3145732 | tf_op jit(solution)/shard_map/while/body/eval_jaxpr/cond
  430.4 7.5 %copy-start.1 = (f32[16,256,64]{1,2,0:T(8,128)S(1)}, f32[16,256,64]{1,2,0:T(8,128)}, u32[]{:S(2)}) copy-start(f32[16,256,64]{1,2,0:T(8,128)} %get-tuple-element.256) | copy-start | bytes 3145732 | tf_op jit(solution)/shard_map/while/body/eval_jaxpr/cond
  430.4 7.5 %copy-start.5 = (bf16[512,16,64]{0,2,1:T(8,128)(2,1)S(1)}, bf16[512,16,64]{0,2,1:T(8,128)(2,1)}, u32[]{:S(2)}) copy-start(bf16[512,16,64]{0,2,1:T(8,128)(2,1)} %get-tuple-element.257) | copy-start | bytes 3145732 | tf_op jit(solution)/shard_map/while/body/eval_jaxpr/cond
  462.2 7.5 %copy-start.1 = (f32[16,256,64]{1,2,0:T(8,128)S(1)}, f32[16,256,64]{1,2,0:T(8,128)}, u32[]{:S(2)}) copy-start(f32[16,256,64]{1,2,0:T(8,128)} %get-tuple-element.256) | copy-start | bytes 3145732 | tf_op jit(solution)/shard_map/while/body/eval_jaxpr/cond
  462.2 7.5 %copy-start.5 = (bf16[512,16,64]{0,2,1:T(8,128)(2,1)S(1)}, bf16[512,16,64]{0,2,1:T(8,128)(2,1)}, u32[]{:S(2)}) copy-start(bf16[512,16,64]{0,2,1:T(8,128)(2,1)} %get-tuple-element.257) | copy-start | bytes 3145732 | tf_op jit(solution)/shard_map/while/body/eval_jaxpr/cond
  493.9 7.5 %copy-start.1 = (f32[16,256,64]{1,2,0:T(8,128)S(1)}, f32[16,256,64]{1,2,0:T(8,128)}, u32[]{:S(2)}) copy-start(f32[16,256,64]{1,2,0:T(8,128)} %get-tuple-element.256) | copy-start | bytes 3145732 | tf_op jit(solution)/shard_map/while/body/eval_jaxpr/cond
  493.9 7.5 %copy-start.5 = (bf16[512,16,64]{0,2,1:T(8,128)(2,1)S(1)}, bf16[512,16,64]{0,2,1:T(8,128)(2,1)}, u32[]{:S(2)}) copy-start(bf16[512,16,64]{0,2,1:T(8,128)(2,1)} %get-tuple-element.257) | copy-start | bytes 3145732 | tf_op jit(solution)/shard_map/while/body/eval_jaxpr/cond
  525.6 7.5 %copy-start.1 = (f32[16,256,64]{1,2,0:T(8,128)S(1)}, f32[16,256,64]{1,2,0:T(8,128)}, u32[]{:S(2)}) copy-start(f32[16,256,64]{1,2,0:T(8,128)} %get-tuple-element.256) | copy-start | bytes 3145732 | tf_op jit(solution)/shard_map/while/body/eval_jaxpr/cond
  525.6 7.5 %copy-start.5 = (bf16[512,16,64]{0,2,1:T(8,128)(2,1)S(1)}, bf16[512,16,64]{0,2,1:T(8,128)(2,1)}, u32[]{:S(2)}) copy-start(bf16[512,16,64]{0,2,1:T(8,128)(2,1)} %get-tuple-element.257) | copy-start | bytes 3145732 | tf_op jit(solution)/shard_map/while/body/eval_jaxpr/cond
  557.4 7.5 %copy-start.1 = (f32[16,256,64]{1,2,0:T(8,128)S(1)}, f32[16,256,64]{1,2,0:T(8,128)}, u32[]{:S(2)}) copy-start(f32[16,256,64]{1,2,0:T(8,128)} %get-tuple-element.256) | copy-start | bytes 3145732 | tf_op jit(solution)/shard_map/while/body/eval_jaxpr/cond
  557.4 7.5 %copy-start.5 = (bf16[512,16,64]{0,2,1:T(8,128)(2,1)S(1)}, bf16[512,16,64]{0,2,1:T(8,128)(2,1)}, u32[]{:S(2)}) copy-start(bf16[512,16,64]{0,2,1:T(8,128)(2,1)} %get-tuple-element.257) | copy-start | bytes 3145732 | tf_op jit(solution)/shard_map/while/body/eval_jaxpr/cond
  572.9 5.9 copy-start.7
  572.9 5.9 copy-start.9
  579.2 14.5 %collective-permute-start.1 = (bf16[256,1024]{1,0:T(8,128)(2,1)S(1)}, bf16[256,1024]{1,0:T(8,128)(2,1)S(1)}, u32[]{:S(2)}, u32[]{:S(2)}) collective-permute-start(bf16[256,1024]{1,0:T(8,128)(2,1)S(1)} %get-tuple-element.382), channel_id=1, source_target_pairs={{0,16},{1,17},{2,18},{3,19},{4,20},{5,21},{6,22},{7,23},{8,24},{9,... | collective-permute-start | bytes 1572872 | tf_op jit(solution)/shard_map/ppermute | solution.py:15
  (18 other events, 37.8 us)
Sparse Core Ops, SparseCore 0:
  109.2 153.5 all-gather.1
where the time goes:
time: 608 us; the launch traced here: 602 us
  waiting for transfers between devices  170 us (28%)
  local copies, waits for them, and re-layouts  167 us (27%)
  other arithmetic  115 us (19%)
  matrix products  85.1 us (14%)
  loops' own time  21.4 us (4%)
  blocking collectives  18 us (3%)
  between operations  13.6 us (2%)
  starting transfers between devices  11.5 us (2%)
    all_gather x1, waiting for transfers between devices, in_one_piece(): lax.all_gather(both, axis, axis=dim, tiled=True)  123 us
    dynamic_slice x16, local copies, waits for them, and re-layouts, one_block(): lax.dynamic_slice_in_dim(value_piece, offset, step_rows, 0)  42.7 us
    another operation x36, other arithmetic, one_block(): jnp.stack([updated[0][slot], updated[1][slot]])  39.4 us
    reduce_sum x12, other arithmetic, fold_block(): denominator = denominator * correction + jnp.sum(raised, axis=-1)  38.8 us
    dot_general x12, matrix products, fold_block(): jnp.einsum('hrk,khd->hrd', raised.astype(jnp.bfloat16), value_block, pref...  37.8 us
    dot_general x12, matrix products, fold_block(): jnp.einsum('rhd,khd->hrk', query_part, key_block, preferred_element_type=...  34.8 us
    ppermute x2, waiting for transfers between devices, from_partner(): return lax.ppermute(value, axis, pairs)  30.2 us
    squeeze x16, local copies, waits for them, and re-layouts, one_block(): part_state = tuple((member[part_index] for member in fold_state))  26.5 us
  transfers between devices with their start and end apart: 4, of which 4 were waited for; matrix products, arithmetic and copies ran while one was open for 2% of the time, Pallas kernels for 0%

commit v1 on v0

--- a/solution.py
+++ b/solution.py
@@ -106,13 +106,10 @@
     my_rank = lax.axis_index("mp")
     tokens_here = byte_states.shape[1]
     half_rows = tokens_here // 2
-    regrouped = lax.all_to_all(
-        lax.all_to_all(patch_latents, "seq", split_axis=0, concat_axis=1, tiled=True),
-        "mp",
-        split_axis=1,
-        concat_axis=2,
-        tiled=True,
-    )
+    x = lax.all_to_all(patch_latents, "seq", split_axis=0, concat_axis=1, tiled=True)
+    parts = jnp.split(x, lax.axis_size("mp"), axis=1)
+    got = lax.all_to_all(jnp.stack(parts), "mp", 0, 0)
+    regrouped = jnp.concatenate(got, axis=2)
     projected = jnp.dot(regrouped[0], w_down, preferred_element_type=jnp.float32)
     patch_normed = rms_norm(projected, kv_gain).astype(jnp.bfloat16)
     lengths = patch_lengths[0]

time: 608 us -> 581 us (0.956)
  other arithmetic: 115 us -> 92 us
    unnamed x1 -> x0, other arithmetic: 23.4 us -> none
    all_to_all x2 -> x0, local copies, waits for them, and re-layouts: 18.6 us -> none  [the longest x1 17 us: per_device(): lax.all_to_all(patch_latents, 'seq', split_axis=0, concat_axis=1, tiled=T...]
    unnamed x25 -> x84, local copies, waits for them, and re-layouts: 8.08 us -> 23.3 us
where the time goes in v1:
time: 581 us; the launch traced here: 575 us
  waiting for transfers between devices  170 us (29%)
  local copies, waits for them, and re-layouts  164 us (28%)
  other arithmetic  92 us (16%)
  matrix products  85.1 us (15%)
  loops' own time  20.5 us (4%)
  blocking collectives  18 us (3%)
  between operations  13.8 us (2%)
  starting transfers between devices  11.3 us (2%)
    all_gather x1, waiting for transfers between devices, in_one_piece(): lax.all_gather(both, axis, axis=dim, tiled=True)  123 us
    dynamic_slice x16, local copies, waits for them, and re-layouts, one_block(): lax.dynamic_slice_in_dim(value_piece, offset, step_rows, 0)  42.7 us
    another operation x36, other arithmetic, one_block(): jnp.stack([updated[0][slot], updated[1][slot]])  39.5 us
    reduce_sum x12, other arithmetic, fold_block(): denominator = denominator * correction + jnp.sum(raised, axis=-1)  38.8 us
    dot_general x12, matrix products, fold_block(): jnp.einsum('hrk,khd->hrd', raised.astype(jnp.bfloat16), value_block, pref...  37.8 us
    dot_general x12, matrix products, fold_block(): jnp.einsum('rhd,khd->hrk', query_part, key_block, preferred_element_type=...  34.8 us
    ppermute x2, waiting for transfers between devices, from_partner(): return lax.ppermute(value, axis, pairs)  30.2 us
    squeeze x16, local copies, waits for them, and re-layouts, one_block(): part_state = tuple((member[part_index] for member in fold_state))  26.7 us
  transfers between devices with their start and end apart: 4, of which 4 were waited for; matrix products, arithmetic and copies ran while one was open for 2% of the time, Pallas kernels for 0%

profile of v1, /device:TPU:24, one launch (start us, length us, event | category | flops | bytes accessed | tf_op | source)
XLA Modules:
  0.0 575.0 jit_solution(6680212217001976158)
XLA Ops:
  6.5 18.0 %all_to_all.17 = bf16[4,1024,128]{2,1,0:T(8,128)(2,1)S(1)} all-to-all(bf16[4,1024,128]{2,1,0:T(8,128)(2,1)} %param.17), channel_id=1, replica_groups=mesh['seq'=4,'mp'=32] {'seq'}, dimensions={0} | all-to-all | bytes 2097152 | tf_op jit(solution)/shard_map/all_to_all | solution.py:109
  48.5 10.6 %all-to-all-start.1 = ((bf16[32,1,128,128]{2,3,1,0:T(8,128)(2,1)}), bf16[32,1,128,128]{2,3,1,0:T(8,128)(2,1)S(1)}, u32[]{:S(2)}, u32[]{:S(2)}) async-start(bf16[32,1,128,128]{2,3,1,0:T(8,128)(2,1)} %constant_dynamic-update-slice_fusion), calls=%async_computation.1 | async-start | bytes 2097152 | tf_op jit(solution)/shard_map/all_to_all | solution.py:111
  59.2 17.0 %all-to-all-done.1 = bf16[32,1,128,128]{2,3,1,0:T(8,128)(2,1)S(1)} async-done(((bf16[32,1,128,128]{2,3,1,0:T(8,128)(2,1)}), bf16[32,1,128,128]{2,3,1,0:T(8,128)(2,1)S(1)}, u32[]{:S(2)}, u32[]{:S(2)}) %all-to-all-start.1) | async-done | bytes 1048608 | tf_op jit(solution)/shard_map/all_to_all | solution.py:111
  76.2 4.9 multiply_reduce_fusion.1
  86.3 15.8 %collective-permute-done = bf16[256,1024]{1,0:T(8,128)(2,1)S(1)} collective-permute-done((bf16[256,1024]{1,0:T(8,128)(2,1)}, bf16[256,1024]{1,0:T(8,128)(2,1)S(1)}, u32[]{:S(2)}, u32[]{:S(2)}) %collective-permute-start) | collective-permute-done | bytes 524320 | tf_op jit(solution)/shard_map/ppermute | solution.py:15
  102.1 4.0 convolution_convert_fusion
  106.1 4.0 reshape.141
  110.1 3.5 copy.56
  113.6 123.1 %all-gather.2.cloned.1.call-done = bf16[4096,2048]{1,0:T(8,128)(2,1)} async-done(((bf16[128,2048]{1,0:T(8,128)(2,1)}), bf16[4096,2048]{1,0:T(8,128)(2,1)}) %all-gather.2.cloned.1.call-update) | async-done | bytes 16777232 | tf_op jit(solution)/shard_map/all_gather | solution.py:20
  236.7 11.6 %fusion.38 = (bf16[4096,1024]{1,0:T(8,128)(2,1)}, bf16[4096,1024]{1,0:T(8,128)(2,1)}) fusion(bf16[4096,2048]{1,0:T(8,128)(2,1)} %all-gather.2.cloned.1.call-done), kind=kLoop, calls=%fused_computation.101 | loop fusion | bytes 33554432 | tf_op jit(solution)/shard_map/slice | solution.py:22
  250.0 296.3 %while.17 = (s32[]{:T(128)}, f32[2,16,256]{2,1,0:T(8,128)S(1)}, f32[2,16,256]{2,1,0:T(8,128)S(1)}, f32[2,16,256,64]{2,3,1,0:T(8,128)}, s32[4096]{0:T(1024)S(1)},...) while((s32[]{:T(128)}, f32[2,16,256]{2,1,0:T(8,128)S(1)}, ...), condition=%wide.region_12.13_spmd, body=%wide.region_3.12_spmd.sunk | while | flops 1130135552 | bytes 99363408 | solution.py:88
  263.2 10.8 %conditional.5 = (f32[1,16,256]{2,1,0:T(8,128)}, f32[1,16,256]{2,1,0:T(8,128)S(1)}, f32[1,16,256,64]{2,3,1,0:T(8,128)S(1)}) conditional(s32[]{:T(128)} %bitcast.151, (f32[16,256]{1,0:T(8,128)}, f32[16,256]{1,0:T(8,128)S(1)}, f32[16,256,64]{1,2,0:T(8,128)S(1)}) %tuple.162, (s32[512]{0:T(512)S(1)}, s32[256]{0:T(256)S(1)}, ...), branch_computations={%region_4.4_spmd, %region_5.0_spmd} | conditional | flops 564797440 | bytes 34835508 | solution.py:85
  266.9 3.2 fusion.2
  276.7 11.9 %conditional.4 = (f32[1,16,256]{2,1,0:T(8,128)}, f32[1,16,256]{2,1,0:T(8,128)S(1)}, f32[1,16,256,64]{2,3,1,0:T(8,128)}) conditional(s32[]{:T(128)} %bitcast.148, (f32[16,256]{1,0:T(8,128)}, f32[16,256]{1,0:T(8,128)S(1)}, f32[16,256,64]{1,2,0:T(8,128)}) %tuple.160, (s32[512]{0:T(512)S(1)}, s32[256]{0:T(256)S(1)}, bf16[2,256,16,64]{1,3,2,0:T(8,128)(2,1)}, ...), branch_computations={%region_8.8_spmd, %region_9.0_spmd} | conditional | flops 564797440 | bytes 43224172 | solution.py:85
  305.7 10.8 %conditional.5 = (f32[1,16,256]{2,1,0:T(8,128)}, f32[1,16,256]{2,1,0:T(8,128)S(1)}, f32[1,16,256,64]{2,3,1,0:T(8,128)S(1)}) conditional(s32[]{:T(128)} %bitcast.151, (f32[16,256]{1,0:T(8,128)}, f32[16,256]{1,0:T(8,128)S(1)}, f32[16,256,64]{1,2,0:T(8,128)S(1)}) %tuple.162, (s32[512]{0:T(512)S(1)}, s32[256]{0:T(256)S(1)}, ...), branch_computations={%region_4.4_spmd, %region_5.0_spmd} | conditional | flops 564797440 | bytes 34835508 | solution.py:85
  309.3 3.2 fusion.2
  319.1 11.9 %conditional.4 = (f32[1,16,256]{2,1,0:T(8,128)}, f32[1,16,256]{2,1,0:T(8,128)S(1)}, f32[1,16,256,64]{2,3,1,0:T(8,128)}) conditional(s32[]{:T(128)} %bitcast.148, (f32[16,256]{1,0:T(8,128)}, f32[16,256]{1,0:T(8,128)S(1)}, f32[16,256,64]{1,2,0:T(8,128)}) %tuple.160, (s32[512]{0:T(512)S(1)}, s32[256]{0:T(256)S(1)}, bf16[2,256,16,64]{1,3,2,0:T(8,128)(2,1)}, ...), branch_computations={%region_8.8_spmd, %region_9.0_spmd} | conditional | flops 564797440 | bytes 43224172 | solution.py:85
  348.1 10.8 %conditional.5 = (f32[1,16,256]{2,1,0:T(8,128)}, f32[1,16,256]{2,1,0:T(8,128)S(1)}, f32[1,16,256,64]{2,3,1,0:T(8,128)S(1)}) conditional(s32[]{:T(128)} %bitcast.151, (f32[16,256]{1,0:T(8,128)}, f32[16,256]{1,0:T(8,128)S(1)}, f32[16,256,64]{1,2,0:T(8,128)S(1)}) %tuple.162, (s32[512]{0:T(512)S(1)}, s32[256]{0:T(256)S(1)}, ...), branch_computations={%region_4.4_spmd, %region_5.0_spmd} | conditional | flops 564797440 | bytes 34835508 | solution.py:85
  351.8 3.2 fusion.2
  361.6 11.9 %conditional.4 = (f32[1,16,256]{2,1,0:T(8,128)}, f32[1,16,256]{2,1,0:T(8,128)S(1)}, f32[1,16,256,64]{2,3,1,0:T(8,128)}) conditional(s32[]{:T(128)} %bitcast.148, (f32[16,256]{1,0:T(8,128)}, f32[16,256]{1,0:T(8,128)S(1)}, f32[16,256,64]{1,2,0:T(8,128)}) %tuple.160, (s32[512]{0:T(512)S(1)}, s32[256]{0:T(256)S(1)}, bf16[2,256,16,64]{1,3,2,0:T(8,128)(2,1)}, ...), branch_computations={%region_8.8_spmd, %region_9.0_spmd} | conditional | flops 564797440 | bytes 43224172 | solution.py:85
  365.3 3.2 fusion.20
  390.5 10.8 %conditional.5 = (f32[1,16,256]{2,1,0:T(8,128)}, f32[1,16,256]{2,1,0:T(8,128)S(1)}, f32[1,16,256,64]{2,3,1,0:T(8,128)S(1)}) conditional(s32[]{:T(128)} %bitcast.151, (f32[16,256]{1,0:T(8,128)}, f32[16,256]{1,0:T(8,128)S(1)}, f32[16,256,64]{1,2,0:T(8,128)S(1)}) %tuple.162, (s32[512]{0:T(512)S(1)}, s32[256]{0:T(256)S(1)}, ...), branch_computations={%region_4.4_spmd, %region_5.0_spmd} | conditional | flops 564797440 | bytes 34835508 | solution.py:85
  404.0 11.9 %conditional.4 = (f32[1,16,256]{2,1,0:T(8,128)}, f32[1,16,256]{2,1,0:T(8,128)S(1)}, f32[1,16,256,64]{2,3,1,0:T(8,128)}) conditional(s32[]{:T(128)} %bitcast.148, (f32[16,256]{1,0:T(8,128)}, f32[16,256]{1,0:T(8,128)S(1)}, f32[16,256,64]{1,2,0:T(8,128)}) %tuple.160, (s32[512]{0:T(512)S(1)}, s32[256]{0:T(256)S(1)}, bf16[2,256,16,64]{1,3,2,0:T(8,128)(2,1)}, ...), branch_computations={%region_8.8_spmd, %region_9.0_spmd} | conditional | flops 564797440 | bytes 43224172 | solution.py:85
  407.7 3.2 fusion.20
  435.7 11.9 %conditional.4 = (f32[1,16,256]{2,1,0:T(8,128)}, f32[1,16,256]{2,1,0:T(8,128)S(1)}, f32[1,16,256,64]{2,3,1,0:T(8,128)}) conditional(s32[]{:T(128)} %bitcast.148, (f32[16,256]{1,0:T(8,128)}, f32[16,256]{1,0:T(8,128)S(1)}, f32[16,256,64]{1,2,0:T(8,128)}) %tuple.160, (s32[512]{0:T(512)S(1)}, s32[256]{0:T(256)S(1)}, bf16[2,256,16,64]{1,3,2,0:T(8,128)(2,1)}, ...), branch_computations={%region_8.8_spmd, %region_9.0_spmd} | conditional | flops 564797440 | bytes 43224172 | solution.py:85
  439.4 3.2 fusion.20
  467.3 11.9 %conditional.4 = (f32[1,16,256]{2,1,0:T(8,128)}, f32[1,16,256]{2,1,0:T(8,128)S(1)}, f32[1,16,256,64]{2,3,1,0:T(8,128)}) conditional(s32[]{:T(128)} %bitcast.148, (f32[16,256]{1,0:T(8,128)}, f32[16,256]{1,0:T(8,128)S(1)}, f32[16,256,64]{1,2,0:T(8,128)}) %tuple.160, (s32[512]{0:T(512)S(1)}, s32[256]{0:T(256)S(1)}, bf16[2,256,16,64]{1,3,2,0:T(8,128)(2,1)}, ...), branch_computations={%region_8.8_spmd, %region_9.0_spmd} | conditional | flops 564797440 | bytes 43224172 | solution.py:85
  471.0 3.2 fusion.20
  498.9 11.9 %conditional.4 = (f32[1,16,256]{2,1,0:T(8,128)}, f32[1,16,256]{2,1,0:T(8,128)S(1)}, f32[1,16,256,64]{2,3,1,0:T(8,128)}) conditional(s32[]{:T(128)} %bitcast.148, (f32[16,256]{1,0:T(8,128)}, f32[16,256]{1,0:T(8,128)S(1)}, f32[16,256,64]{1,2,0:T(8,128)}) %tuple.160, (s32[512]{0:T(512)S(1)}, s32[256]{0:T(256)S(1)}, bf16[2,256,16,64]{1,3,2,0:T(8,128)(2,1)}, ...), branch_computations={%region_8.8_spmd, %region_9.0_spmd} | conditional | flops 564797440 | bytes 43224172 | solution.py:85
  502.7 3.2 fusion.20
  530.6 11.9 %conditional.4 = (f32[1,16,256]{2,1,0:T(8,128)}, f32[1,16,256]{2,1,0:T(8,128)S(1)}, f32[1,16,256,64]{2,3,1,0:T(8,128)}) conditional(s32[]{:T(128)} %bitcast.148, (f32[16,256]{1,0:T(8,128)}, f32[16,256]{1,0:T(8,128)S(1)}, f32[16,256,64]{1,2,0:T(8,128)}) %tuple.160, (s32[512]{0:T(512)S(1)}, s32[256]{0:T(256)S(1)}, bf16[2,256,16,64]{1,3,2,0:T(8,128)(2,1)}, ...), branch_computations={%region_8.8_spmd, %region_9.0_spmd} | conditional | flops 564797440 | bytes 43224172 | solution.py:85
  552.7 14.4 %collective-permute-done.1 = bf16[256,1024]{1,0:T(8,128)(2,1)S(1)} collective-permute-done((bf16[256,1024]{1,0:T(8,128)(2,1)S(1)}, bf16[256,1024]{1,0:T(8,128)(2,1)S(1)}, u32[]{:S(2)}, u32[]{:S(2)}) %collective-permute-start.1) | collective-permute-done | bytes 524320 | tf_op jit(solution)/shard_map/ppermute | solution.py:15
  (366 shorter events, 287.8 us)
Async XLA Ops:
  6.5 543.1 %copy-start = (bf16[1024,1024]{1,0:T(8,128)(2,1)S(1)}, bf16[1024,1024]{1,0:T(8,128)(2,1)}, u32[]{:S(2)}) copy-start(bf16[1024,1024]{1,0:T(8,128)(2,1)} %param.24) | copy-start | bytes 6291460
  6.5 52.6 %copy-start.13 = (bf16[1024]{0:T(1024)(128)(2,1)S(1)}, bf16[1024]{0:T(1024)(128)(2,1)}, u32[]{:S(2)}) copy-start(bf16[1024]{0:T(1024)(128)(2,1)} %param.20) | copy-start | bytes 6148
  48.5 27.7 %all-to-all-start.1 = ((bf16[32,1,128,128]{2,3,1,0:T(8,128)(2,1)}), bf16[32,1,128,128]{2,3,1,0:T(8,128)(2,1)S(1)}, u32[]{:S(2)}, u32[]{:S(2)}) async-start(bf16[32,1,128,128]{2,3,1,0:T(8,128)(2,1)} %constant_dynamic-update-slice_fusion), calls=%async_computation.1 | async-start | bytes 2097152 | tf_op jit(solution)/shard_map/all_to_all | solution.py:111
  59.1 177.6 %all-gather.2.cloned.1.call-start = ((), (), s32[]{:S(2)}) async-start(), calls=%async_computation.2 | async-start | bytes 17301504 | tf_op jit(solution)/shard_map/all_gather | solution.py:20
  76.2 5.4 copy-start.11
  81.1 4.9 copy-start.14
  85.1 28.6 %copy-start.6 = (bf16[256,1024]{1,0:T(8,128)(2,1)}, bf16[256,1024]{1,0:T(8,128)(2,1)S(1)}, u32[]{:S(2)}) copy-start(bf16[256,1024]{1,0:T(8,128)(2,1)S(1)} %get-tuple-element.363) | copy-start | bytes 1572868
  85.1 17.0 %collective-permute-start = (bf16[256,1024]{1,0:T(8,128)(2,1)}, bf16[256,1024]{1,0:T(8,128)(2,1)S(1)}, u32[]{:S(2)}, u32[]{:S(2)}) collective-permute-start(bf16[256,1024]{1,0:T(8,128)(2,1)} %get-tuple-element.364), channel_id=1, source_target_pairs={{0,16},{1,17},{2,18},{3,19},{4,20},{5,21},{6,22},{7,23},{8,24},{9,... | collective-permute-start | bytes 1572872 | tf_op jit(solution)/shard_map/ppermute | solution.py:15
  102.1 146.3 %copy-start.8 = (bf16[256,1024]{1,0:T(8,128)(2,1)}, bf16[256,1024]{1,0:T(8,128)(2,1)S(1)}, u32[]{:S(2)}) copy-start(bf16[256,1024]{1,0:T(8,128)(2,1)S(1)} %collective-permute-done) | copy-start | bytes 1572868
  263.4 7.5 %copy-start.4 = (bf16[512,16,64]{0,2,1:T(8,128)(2,1)S(1)}, bf16[512,16,64]{0,2,1:T(8,128)(2,1)}, u32[]{:S(2)}) copy-start(bf16[512,16,64]{0,2,1:T(8,128)(2,1)} %get-tuple-element.249) | copy-start | bytes 3145732 | tf_op jit(solution)/shard_map/while/body/eval_jaxpr/cond
  276.9 7.5 %copy-start.1 = (f32[16,256,64]{1,2,0:T(8,128)S(1)}, f32[16,256,64]{1,2,0:T(8,128)}, u32[]{:S(2)}) copy-start(f32[16,256,64]{1,2,0:T(8,128)} %get-tuple-element.256) | copy-start | bytes 3145732 | tf_op jit(solution)/shard_map/while/body/eval_jaxpr/cond
  276.9 7.5 %copy-start.5 = (bf16[512,16,64]{0,2,1:T(8,128)(2,1)S(1)}, bf16[512,16,64]{0,2,1:T(8,128)(2,1)}, u32[]{:S(2)}) copy-start(bf16[512,16,64]{0,2,1:T(8,128)(2,1)} %get-tuple-element.257) | copy-start | bytes 3145732 | tf_op jit(solution)/shard_map/while/body/eval_jaxpr/cond
  305.8 7.5 %copy-start.4 = (bf16[512,16,64]{0,2,1:T(8,128)(2,1)S(1)}, bf16[512,16,64]{0,2,1:T(8,128)(2,1)}, u32[]{:S(2)}) copy-start(bf16[512,16,64]{0,2,1:T(8,128)(2,1)} %get-tuple-element.249) | copy-start | bytes 3145732 | tf_op jit(solution)/shard_map/while/body/eval_jaxpr/cond
  319.3 7.5 %copy-start.1 = (f32[16,256,64]{1,2,0:T(8,128)S(1)}, f32[16,256,64]{1,2,0:T(8,128)}, u32[]{:S(2)}) copy-start(f32[16,256,64]{1,2,0:T(8,128)} %get-tuple-element.256) | copy-start | bytes 3145732 | tf_op jit(solution)/shard_map/while/body/eval_jaxpr/cond
  319.3 7.5 %copy-start.5 = (bf16[512,16,64]{0,2,1:T(8,128)(2,1)S(1)}, bf16[512,16,64]{0,2,1:T(8,128)(2,1)}, u32[]{:S(2)}) copy-start(bf16[512,16,64]{0,2,1:T(8,128)(2,1)} %get-tuple-element.257) | copy-start | bytes 3145732 | tf_op jit(solution)/shard_map/while/body/eval_jaxpr/cond
  348.3 7.5 %copy-start.4 = (bf16[512,16,64]{0,2,1:T(8,128)(2,1)S(1)}, bf16[512,16,64]{0,2,1:T(8,128)(2,1)}, u32[]{:S(2)}) copy-start(bf16[512,16,64]{0,2,1:T(8,128)(2,1)} %get-tuple-element.249) | copy-start | bytes 3145732 | tf_op jit(solution)/shard_map/while/body/eval_jaxpr/cond
  361.7 7.5 %copy-start.1 = (f32[16,256,64]{1,2,0:T(8,128)S(1)}, f32[16,256,64]{1,2,0:T(8,128)}, u32[]{:S(2)}) copy-start(f32[16,256,64]{1,2,0:T(8,128)} %get-tuple-element.256) | copy-start | bytes 3145732 | tf_op jit(solution)/shard_map/while/body/eval_jaxpr/cond
  361.8 7.5 %copy-start.5 = (bf16[512,16,64]{0,2,1:T(8,128)(2,1)S(1)}, bf16[512,16,64]{0,2,1:T(8,128)(2,1)}, u32[]{:S(2)}) copy-start(bf16[512,16,64]{0,2,1:T(8,128)(2,1)} %get-tuple-element.257) | copy-start | bytes 3145732 | tf_op jit(solution)/shard_map/while/body/eval_jaxpr/cond
  390.7 7.5 %copy-start.4 = (bf16[512,16,64]{0,2,1:T(8,128)(2,1)S(1)}, bf16[512,16,64]{0,2,1:T(8,128)(2,1)}, u32[]{:S(2)}) copy-start(bf16[512,16,64]{0,2,1:T(8,128)(2,1)} %get-tuple-element.249) | copy-start | bytes 3145732 | tf_op jit(solution)/shard_map/while/body/eval_jaxpr/cond
  404.2 7.5 %copy-start.1 = (f32[16,256,64]{1,2,0:T(8,128)S(1)}, f32[16,256,64]{1,2,0:T(8,128)}, u32[]{:S(2)}) copy-start(f32[16,256,64]{1,2,0:T(8,128)} %get-tuple-element.256) | copy-start | bytes 3145732 | tf_op jit(solution)/shard_map/while/body/eval_jaxpr/cond
  404.2 7.5 %copy-start.5 = (bf16[512,16,64]{0,2,1:T(8,128)(2,1)S(1)}, bf16[512,16,64]{0,2,1:T(8,128)(2,1)}, u32[]{:S(2)}) copy-start(bf16[512,16,64]{0,2,1:T(8,128)(2,1)} %get-tuple-element.257) | copy-start | bytes 3145732 | tf_op jit(solution)/shard_map/while/body/eval_jaxpr/cond
  435.8 7.5 %copy-start.1 = (f32[16,256,64]{1,2,0:T(8,128)S(1)}, f32[16,256,64]{1,2,0:T(8,128)}, u32[]{:S(2)}) copy-start(f32[16,256,64]{1,2,0:T(8,128)} %get-tuple-element.256) | copy-start | bytes 3145732 | tf_op jit(solution)/shard_map/while/body/eval_jaxpr/cond
  435.8 7.5 %copy-start.5 = (bf16[512,16,64]{0,2,1:T(8,128)(2,1)S(1)}, bf16[512,16,64]{0,2,1:T(8,128)(2,1)}, u32[]{:S(2)}) copy-start(bf16[512,16,64]{0,2,1:T(8,128)(2,1)} %get-tuple-element.257) | copy-start | bytes 3145732 | tf_op jit(solution)/shard_map/while/body/eval_jaxpr/cond
  467.5 7.5 %copy-start.1 = (f32[16,256,64]{1,2,0:T(8,128)S(1)}, f32[16,256,64]{1,2,0:T(8,128)}, u32[]{:S(2)}) copy-start(f32[16,256,64]{1,2,0:T(8,128)} %get-tuple-element.256) | copy-start | bytes 3145732 | tf_op jit(solution)/shard_map/while/body/eval_jaxpr/cond
  467.5 7.5 %copy-start.5 = (bf16[512,16,64]{0,2,1:T(8,128)(2,1)S(1)}, bf16[512,16,64]{0,2,1:T(8,128)(2,1)}, u32[]{:S(2)}) copy-start(bf16[512,16,64]{0,2,1:T(8,128)(2,1)} %get-tuple-element.257) | copy-start | bytes 3145732 | tf_op jit(solution)/shard_map/while/body/eval_jaxpr/cond
  499.1 7.5 %copy-start.1 = (f32[16,256,64]{1,2,0:T(8,128)S(1)}, f32[16,256,64]{1,2,0:T(8,128)}, u32[]{:S(2)}) copy-start(f32[16,256,64]{1,2,0:T(8,128)} %get-tuple-element.256) | copy-start | bytes 3145732 | tf_op jit(solution)/shard_map/while/body/eval_jaxpr/cond
  499.1 7.5 %copy-start.5 = (bf16[512,16,64]{0,2,1:T(8,128)(2,1)S(1)}, bf16[512,16,64]{0,2,1:T(8,128)(2,1)}, u32[]{:S(2)}) copy-start(bf16[512,16,64]{0,2,1:T(8,128)(2,1)} %get-tuple-element.257) | copy-start | bytes 3145732 | tf_op jit(solution)/shard_map/while/body/eval_jaxpr/cond
  530.8 7.5 %copy-start.1 = (f32[16,256,64]{1,2,0:T(8,128)S(1)}, f32[16,256,64]{1,2,0:T(8,128)}, u32[]{:S(2)}) copy-start(f32[16,256,64]{1,2,0:T(8,128)} %get-tuple-element.256) | copy-start | bytes 3145732 | tf_op jit(solution)/shard_map/while/body/eval_jaxpr/cond
  530.8 7.5 %copy-start.5 = (bf16[512,16,64]{0,2,1:T(8,128)(2,1)S(1)}, bf16[512,16,64]{0,2,1:T(8,128)(2,1)}, u32[]{:S(2)}) copy-start(bf16[512,16,64]{0,2,1:T(8,128)(2,1)} %get-tuple-element.257) | copy-start | bytes 3145732 | tf_op jit(solution)/shard_map/while/body/eval_jaxpr/cond
  546.3 5.9 %copy-start.7 = (bf16[256,1024]{1,0:T(8,128)(2,1)S(1)}, bf16[256,1024]{1,0:T(8,128)(2,1)}, u32[]{:S(2)}) copy-start(bf16[256,1024]{1,0:T(8,128)(2,1)} %copy-done.6) | copy-start | bytes 1572868
  546.3 5.9 %copy-start.9 = (bf16[256,1024]{1,0:T(8,128)(2,1)S(1)}, bf16[256,1024]{1,0:T(8,128)(2,1)}, u32[]{:S(2)}) copy-start(bf16[256,1024]{1,0:T(8,128)(2,1)} %copy-done.8) | copy-start | bytes 1572868
  552.6 14.5 %collective-permute-start.1 = (bf16[256,1024]{1,0:T(8,128)(2,1)S(1)}, bf16[256,1024]{1,0:T(8,128)(2,1)S(1)}, u32[]{:S(2)}, u32[]{:S(2)}) collective-permute-start(bf16[256,1024]{1,0:T(8,128)(2,1)S(1)} %get-tuple-element.362), channel_id=1, source_target_pairs={{0,16},{1,17},{2,18},{3,19},{4,20},{5,21},{6,22},{7,23},{8,24},{9,... | collective-permute-start | bytes 1572872 | tf_op jit(solution)/shard_map/ppermute | solution.py:15
  (18 other events, 38.8 us)
Sparse Core Ops, SparseCore 0:
  83.1 153.5 all-gather.1
